TPU v7x, 256 devices: a 2x2x32 block of a 4x8x32 slice. The times are simulated.
256 devices in a mesh: batch: 4 (over x, y), rows: 64 (over z, core).
Axes of the slice: x: 2, y: 2, z: 32, core: 2. Of those that a mesh axis runs over, the one named last changes fastest.
The devices are a block of a 4x8x32 slice.
Arguments:
- latent: bfloat16 [16, 1536, 256], P(None, ('batch', 'rows')), parts along dimension 1, may hold values from -11 to 11
- kernel_in: bfloat16 [3, 3, 16, 512], replicated, may hold values from -0.5 to 0.5
- gain_one: float32 [512], replicated, may hold values from 0.25 to 1.75
- bias_one: float32 [512], replicated, may hold values from -3 to 3
- kernel_one: bfloat16 [3, 3, 512, 512], replicated, may hold values from -0.09375 to 0.09375
- gain_two: float32 [512], replicated, may hold values from 0.25 to 1.75
- bias_two: float32 [512], replicated, may hold values from -3 to 3
- kernel_two: bfloat16 [3, 3, 512, 512], replicated, may hold values from -0.09375 to 0.09375
Outputs:
- block_out: bfloat16 [1536, 256, 512], P(('batch', 'rows')), parts along dimension 0
There are 4 independent parts, one for each index of `batch`. A program takes and returns all parts, laid end to end along the dimension named above; an argument that names none is the same for every part. Nothing has to cross between parts.
All inputs are finite; a program needn't handle non-finite values.
Results may differ from a plain program's by a relative error of at most 0.014.
Values may be sent and summed in bfloat16 or wider, within the bound.
No kernel may reach another device: no remote copies, remote signals or barrier semaphores. Data moves between devices by JAX's collectives and lax.ppermute only.
A program may use at most 64 MiB of HBM per device.

v0:
```python
import jax
import jax.numpy as jnp
from jax import lax
from jax.sharding import PartitionSpec as P

GROUPS = 32


EPSILON = 1e-06


def sent_to_all(shard, axis):
    copies = jnp.broadcast_to(shard, (lax.axis_size(axis), *shard.shape))
    return lax.all_to_all(copies, axis, split_axis=0, concat_axis=0, tiled=True)


def over_copies(shard, axis):
    return sent_to_all(shard, axis).sum(axis=0)


def in_one(arrays, axis):
    line, at, done = (jnp.concatenate([a.reshape(-1) for a in arrays]), 0, [])
    running = over_copies(line, axis)
    for a in arrays:
        done.append(running[at : at + a.size].reshape(a.shape))
        at += a.size
    return tuple(done)


def extended(cells, sides, width):
    for axis, dim in sides:
        count = lax.axis_size(axis)
        ends = count - 1
        head = lax.slice_in_dim(cells, 0, width, axis=dim)
        tail = lax.slice_in_dim(cells, cells.shape[dim] - width, cells.shape[dim], axis=dim)
        cells = jnp.concatenate(
            [
                lax.ppermute(tail, axis, [(i, (i + 1) % count) for i in range(ends)]),
                cells,
                lax.ppermute(head, axis, [((i + 1) % count, i) for i in range(ends)]),
            ],
            axis=dim,
        )
    return cells


def convolve(padded, kernel):
    height = padded.shape[0] - 2
    width = padded.shape[1] - 2
    inputs = padded.shape[2]
    total = jnp.zeros((height * width, kernel.shape[3]), jnp.float32)
    for row_shift in range(3):
        band = padded[row_shift : row_shift + height]
        stacked = jnp.concatenate(
            [band[:, col_shift : col_shift + width] for col_shift in range(3)], axis=-1
        )
        total = total + jnp.dot(
            stacked.reshape(height * width, 3 * inputs),
            kernel[row_shift].reshape(3 * inputs, -1),
            preferred_element_type=jnp.float32,
        )
    return total.reshape(height, width, -1)


def pad_columns(field):
    return jnp.pad(field, ((0, 0), (1, 1), (0, 0)))


def moments(own):
    values = own.astype(jnp.float32).reshape(own.shape[0], own.shape[1], GROUPS, -1)
    count = values.shape[0] * values.shape[1] * values.shape[3] * lax.axis_size("rows")
    totals, squares = in_one(
        (jnp.sum(values, axis=(0, 1, 3)), jnp.sum(values * values, axis=(0, 1, 3))), "rows"
    )
    center = totals / count
    spread = squares / count - center * center
    return (center, spread)


def activate(field, center, spread, gain, bias):
    values = field.astype(jnp.float32).reshape(field.shape[0], field.shape[1], GROUPS, -1)
    normed = (values - center[None, None, :, None]) * lax.rsqrt(spread + EPSILON)[
        None, None, :, None
    ]
    normed = normed.reshape(field.shape) * gain + bias
    return jax.nn.silu(normed).astype(jnp.bfloat16)


def inside(field, margin, rows_dev):
    first_row = lax.axis_index("rows") * rows_dev - margin
    global_rows = first_row + jnp.arange(field.shape[0], dtype=jnp.int32)
    valid = (global_rows >= 0) & (global_rows < rows_dev * lax.axis_size("rows"))
    return jnp.where(valid[:, None, None], field, jnp.zeros_like(field))


def local(latent, kernel_in, gain_one, bias_one, kernel_one, gain_two, bias_two, kernel_two):
    rows_dev = latent.shape[1]
    padded = extended(latent, (("rows", 1),), 3)
    wide = convolve(pad_columns(jnp.transpose(padded, (1, 2, 0))), kernel_in).astype(jnp.bfloat16)
    features = wide[2 : 2 + rows_dev]
    center, spread = moments(features)
    first = inside(activate(wide, center, spread, gain_one, bias_one), 2, rows_dev)
    hidden_wide = convolve(pad_columns(first), kernel_one).astype(jnp.bfloat16)
    center, spread = moments(hidden_wide[1 : 1 + rows_dev])
    second = inside(activate(hidden_wide, center, spread, gain_two, bias_two), 1, rows_dev)
    result = features.astype(jnp.float32) + convolve(pad_columns(second), kernel_two)
    return result.astype(jnp.bfloat16)


def solution(mesh):
    in_specs = (P(None, ("batch", "rows"), None), P(), P(), P(), P(), P(), P(), P())
    out_specs = P(("batch", "rows"), None, None)
    return jax.shard_map(local, mesh=mesh, in_specs=in_specs, out_specs=out_specs, check_vma=False)
```

profile of v0, /device:TPU:37, one launch (start us, length us, event | category | flops | bytes accessed | tf_op | source)
XLA Modules:
  0.0 150.6 jit_solution(15982491090367136540)
XLA Ops:
  0.0 0.8 fusion.26
  0.8 5.1 %collective-permute-start = (bf16[16,3,256]{2,0,1:T(8,128)(2,1)S(1)}, bf16[16,3,256]{2,0,1:T(8,128)(2,1)S(1)}, u32[]{:S(2)}, u32[]{:S(2)}) collective-permute-start(bf16[16,3,256]{2,0,1:T(8,128)(2,1)S(1)} %get-tuple-element.45), channel_id=1, source_target_pairs={{0,1},{1,2},{2,3},{3,4},{4,5},{5,6},{6,7},{7,8},{8,9},{9,10},{10,1... | collective-permute-start | bytes 73736 | tf_op jit(solution)/shard_map/ppermute | solution.py:38
  5.8 18.6 %collective-permute-start.1 = (bf16[16,3,256]{2,0,1:T(8,128)(2,1)S(1)}, bf16[16,3,256]{2,0,1:T(8,128)(2,1)S(1)}, u32[]{:S(2)}, u32[]{:S(2)}) collective-permute-start(bf16[16,3,256]{2,0,1:T(8,128)(2,1)S(1)} %get-tuple-element.46), channel_id=1, source_target_pairs={{1,0},{2,1},{3,2},{4,3},{5,4},{6,5},{7,6},{8,7},{9,8},{10,9},{11,1... | collective-permute-start | bytes 73736 | tf_op jit(solution)/shard_map/ppermute | solution.py:40
  24.4 0.9 fusion.25
  25.3 0.8 maximum_bitcast_fusion.3
  26.5 0.9 fusion.27
  27.3 0.9 fusion.28
  28.2 0.9 add_convert_fusion
  30.7 18.4 %all-to-all-start = ((f32[64,1,64]{2,1,0:T(1,128)}), f32[64,1,64]{2,1,0:T(1,128)S(1)}, u32[]{:S(2)}, u32[]{:S(2)}) async-start(f32[64,1,64]{2,1,0:T(1,128)} %broadcast_in_dim.40), calls=%async_computation | async-start | bytes 65536 | tf_op jit(solution)/shard_map/all_to_all | solution.py:14
  49.1 4.7 %fusion.24 = (bf16[1,3,512,512]{3,2,1,0:T(8,128)(2,1)}, bf16[1,3,512,512]{3,2,1,0:T(8,128)(2,1)}, bf16[1,3,512,512]{3,2,1,0:T(8,128)(2,1)}) fusion(bf16[3,3,512,512]{3,2,1,0:T(8,128)(2,1)} %param.12), kind=kLoop, calls=%fused_computation.71 | loop fusion | bytes 9437184 | tf_op jit(solution)/shard_map/slice | solution.py:59
  53.8 17.1 %all-to-all-done = f32[64,1,64]{2,1,0:T(1,128)S(1)} async-done(((f32[64,1,64]{2,1,0:T(1,128)}), f32[64,1,64]{2,1,0:T(1,128)S(1)}, u32[]{:S(2)}, u32[]{:S(2)}) %all-to-all-start) | async-done | bytes 16416 | tf_op jit(solution)/shard_map/all_to_all | solution.py:14
  71.3 2.0 %fusion.21 = bf16[10,256,512]{2,1,0:T(8,128)(2,1)S(1)} fusion(bf16[10,256,512]{2,1,0:T(8,128)(2,1)S(1)} %bitcast.51, f32[512]{0:T(512)S(1)} %copy-done.9, f32[512]{0:T(512)S(1)} %copy-done.10, f32[512]{0:T(512)S(1)} %mul.74, f32[512]{0:T(512)S(1)} %sub.41, pred[10]{0:T(512)(128)(4,1)S(1)} %compare_and_fusion), kind=kLoop, calls=%fused_computation.38 | loop fusion | flops 14417920 | bytes 5251082 | tf_op jit(solution)/shard_map/jit(_where)/select_n | solution.py:93
  73.4 9.1 %pad_slice_fusion.1 = (bf16[8,256,512]{2,1,0:T(8,128)(2,1)S(1)}, bf16[8,256,512]{2,1,0:T(8,128)(2,1)S(1)}, bf16[8,256,512]{2,1,0:T(8,128)(2,1)S(1)}, bf16[8,256,...) fusion(bf16[10,256,512]{2,1,0:T(8,128)(2,1)S(1)} %fusion.21), kind=kLoop, calls=%fused_computation.41 | loop fusion | bytes 27787264 | tf_op jit(solution)/shard_map/slice | solution.py:55
  82.5 3.3 %pad_maximum_fusion.1 = bf16[8,256,1536]{2,1,0:T(8,128)(2,1)S(1)} fusion(bf16[8,256,512]{2,1,0:T(8,128)(2,1)} %get-tuple-element.18, bf16[8,256,512]{2,1,0:T(8,128)(2,1)} %get-tuple-element.21, bf16[8,256,512]{2,1,0:T(8,128)(2,1)S(1)} %get-tuple-element.17), kind=kLoop, calls=%fused_computation.1 | loop fusion | flops 18874368 | bytes 12582912 | tf_op jit(solution)/shard_map/concatenate | solution.py:54
  85.8 3.4 %fusion.30 = f32[2048,512]{1,0:T(8,128)S(1)} fusion(bf16[2048,1536]{1,0:T(8,128)(2,1)S(1)} %bitcast.54, bf16[1536,512]{1,0:T(8,128)(2,1)S(1)} %bitcast.63), kind=kOutput, calls=%fused_computation.77 | convolution fusion | flops 3221225472 | bytes 12058624 | tf_op jit(solution)/shard_map/dot_general | solution.py:57
  89.2 0.8 pad_maximum_fusion
  90.6 3.5 %fusion.29 = f32[2048,512]{1,0:T(8,128)S(1)} fusion(bf16[2048,1536]{1,0:T(8,128)(2,1)S(1)} %bitcast.55, bf16[1536,512]{1,0:T(8,128)(2,1)S(1)} %bitcast.61), kind=kOutput, calls=%fused_computation.76 | convolution fusion | flops 3221225472 | bytes 12058624 | tf_op jit(solution)/shard_map/dot_general | solution.py:57
  94.2 0.7 pad_maximum_fusion.2
  94.9 0.7 copy-done.3
  95.6 3.8 %add_convert_fusion.1 = bf16[2048,512]{1,0:T(8,128)(2,1)S(1)} fusion(f32[2048,512]{1,0:T(8,128)S(1)} %fusion.29, f32[2048,512]{1,0:T(8,128)S(1)} %fusion.30, bf16[2048,1536]{1,0:T(8,128)(2,1)S(1)} %bitcast.53, bf16[1536,512]{1,0:T(8,128)(2,1)S(1)} %bitcast.59), kind=kOutput, calls=%fused_computation.30 | convolution fusion | flops 3224371200 | bytes 18350080 | tf_op jit(solution)/shard_map/dot_general | solution.py:57
  99.4 1.3 copy-done.2
  101.7 0.6 broadcast_in_dim.42
  102.3 6.5 %all-to-all-start.1 = ((f32[64,1,64]{2,1,0:T(1,128)}), f32[64,1,64]{2,1,0:T(1,128)S(1)}, u32[]{:S(2)}, u32[]{:S(2)}) async-start(f32[64,1,64]{2,1,0:T(1,128)} %broadcast_in_dim.42), calls=%async_computation.1 | async-start | bytes 65536 | tf_op jit(solution)/shard_map/all_to_all | solution.py:14
  108.8 4.7 %fusion.23 = (bf16[1,3,512,512]{3,2,1,0:T(8,128)(2,1)}, bf16[1,3,512,512]{3,2,1,0:T(8,128)(2,1)}, bf16[1,3,512,512]{3,2,1,0:T(8,128)(2,1)}) fusion(bf16[3,3,512,512]{3,2,1,0:T(8,128)(2,1)} %param.15), kind=kLoop, calls=%fused_computation.70 | loop fusion | bytes 9437184 | tf_op jit(solution)/shard_map/slice | solution.py:59
  113.5 18.0 %all-to-all-done.1 = f32[64,1,64]{2,1,0:T(1,128)S(1)} async-done(((f32[64,1,64]{2,1,0:T(1,128)}), f32[64,1,64]{2,1,0:T(1,128)S(1)}, u32[]{:S(2)}, u32[]{:S(2)}) %all-to-all-start.1) | async-done | bytes 16416 | tf_op jit(solution)/shard_map/all_to_all | solution.py:14
  132.0 3.2 %fusion.22 = bf16[8,256,512]{2,1,0:T(8,128)(2,1)S(1)} fusion(bf16[8,256,512]{2,1,0:T(8,128)(2,1)} %bitcast.52, f32[512]{0:T(512)S(1)} %copy-done.11, f32[512]{0:T(512)S(1)} %copy-done.12, f32[512]{0:T(512)S(1)} %mul.83, f32[512]{0:T(512)S(1)} %sub.46, pred[8]{0:T(512)(128)(4,1)S(1)} %compare_and_fusion.1), kind=kLoop, calls=%fused_computation.39 | loop fusion | flops 11534336 | bytes 4202504 | tf_op jit(solution)/shard_map/jit(_where)/select_n | solution.py:93
  135.1 3.2 %pad_slice_fusion.7 = (bf16[6,256,512]{2,1,0:T(8,128)(2,1)S(1)}, bf16[6,256,512]{2,1,0:T(8,128)(2,1)S(1)}, bf16[6,256,512]{2,1,0:T(8,128)(2,1)S(1)}, bf16[6,256,...) fusion(bf16[8,256,512]{2,1,0:T(8,128)(2,1)S(1)} %fusion.22), kind=kLoop, calls=%fused_computation.47 | loop fusion | bytes 20971520 | tf_op jit(solution)/shard_map/slice | solution.py:55
  138.9 0.9 copy-done.8
  139.8 2.6 %fusion.31 = f32[1536,512]{1,0:T(8,128)S(1)} fusion(bf16[1536,1536]{1,0:T(8,128)(2,1)S(1)} %bitcast.58, bf16[1536,512]{1,0:T(8,128)(2,1)S(1)} %bitcast.64), kind=kOutput, calls=%fused_computation.78 | convolution fusion | flops 2415919104 | bytes 9437184 | tf_op jit(solution)/shard_map/dot_general | solution.py:57
  143.4 0.9 copy-done.6
  144.3 2.6 %convolution_add_fusion.1 = f32[1536,512]{1,0:T(8,128)S(1)} fusion(f32[1536,512]{1,0:T(8,128)S(1)} %fusion.31, bf16[1536,1536]{1,0:T(8,128)(2,1)S(1)} %bitcast.57, bf16[1536,512]{1,0:T(8,128)(2,1)S(1)} %bitcast.62), kind=kOutput, calls=%fused_computation.34 | convolution fusion | flops 2416705536 | bytes 12582912 | tf_op jit(solution)/shard_map/dot_general | solution.py:57
  146.9 3.7 %fusion.20 = bf16[1536,512]{1,0:T(8,128)(2,1)} fusion(f32[1536,512]{1,0:T(8,128)S(1)} %convolution_add_fusion.1, bf16[1536,1536]{1,0:T(8,128)(2,1)S(1)} %bitcast.56, bf16[1536,512]{1,0:T(8,128)(2,1)S(1)} %bitcast.60, bf16[2560,512]{1,0:T(8,128)(2,1)S(1)} %add_convert_fusion), kind=kOutput, calls=%fused_computation.37 | convolution fusion | flops 2419064832 | bytes 12582912 | tf_op jit(solution)/shard_map/dot_general | solution.py:57
  (60 shorter events, 5.7 us)
Async XLA Ops:
  0.8 24.5 %collective-permute-start = (bf16[16,3,256]{2,0,1:T(8,128)(2,1)S(1)}, bf16[16,3,256]{2,0,1:T(8,128)(2,1)S(1)}, u32[]{:S(2)}, u32[]{:S(2)}) collective-permute-start(bf16[16,3,256]{2,0,1:T(8,128)(2,1)S(1)} %get-tuple-element.45), channel_id=1, source_target_pairs={{0,1},{1,2},{2,3},{3,4},{4,5},{5,6},{6,7},{7,8},{8,9},{9,10},{10,1... | collective-permute-start | bytes 73736 | tf_op jit(solution)/shard_map/ppermute | solution.py:38
  5.8 19.5 %collective-permute-start.1 = (bf16[16,3,256]{2,0,1:T(8,128)(2,1)S(1)}, bf16[16,3,256]{2,0,1:T(8,128)(2,1)S(1)}, u32[]{:S(2)}, u32[]{:S(2)}) collective-permute-start(bf16[16,3,256]{2,0,1:T(8,128)(2,1)S(1)} %get-tuple-element.46), channel_id=1, source_target_pairs={{1,0},{2,1},{3,2},{4,3},{5,4},{6,5},{7,6},{8,7},{9,8},{10,9},{11,1... | collective-permute-start | bytes 73736 | tf_op jit(solution)/shard_map/ppermute | solution.py:40
  30.7 40.2 %all-to-all-start = ((f32[64,1,64]{2,1,0:T(1,128)}), f32[64,1,64]{2,1,0:T(1,128)S(1)}, u32[]{:S(2)}, u32[]{:S(2)}) async-start(f32[64,1,64]{2,1,0:T(1,128)} %broadcast_in_dim.40), calls=%async_computation | async-start | bytes 65536 | tf_op jit(solution)/shard_map/all_to_all | solution.py:14
  49.1 22.2 %copy-start.9 = (f32[512]{0:T(512)S(1)}, f32[512]{0:T(512)}, u32[]{:S(2)}) copy-start(f32[512]{0:T(512)} %param.11) | copy-start | bytes 6148
  49.1 22.2 %copy-start.10 = (f32[512]{0:T(512)S(1)}, f32[512]{0:T(512)}, u32[]{:S(2)}) copy-start(f32[512]{0:T(512)} %param.10) | copy-start | bytes 6148
  82.5 3.3 %copy-start.7 = (bf16[1,3,512,512]{3,2,1,0:T(8,128)(2,1)S(1)}, bf16[1,3,512,512]{3,2,1,0:T(8,128)(2,1)}, u32[]{:S(2)}) copy-start(bf16[1,3,512,512]{3,2,1,0:T(8,128)(2,1)} %get-tuple-element.14) | copy-start | bytes 4718596
  85.7 3.5 %copy-start = (bf16[8,256,512]{2,1,0:T(8,128)(2,1)S(1)}, bf16[8,256,512]{2,1,0:T(8,128)(2,1)}, u32[]{:S(2)}) copy-start(bf16[8,256,512]{2,1,0:T(8,128)(2,1)} %get-tuple-element.22) | copy-start | bytes 6291460
  85.7 3.5 %copy-start.1 = (bf16[8,256,512]{2,1,0:T(8,128)(2,1)S(1)}, bf16[8,256,512]{2,1,0:T(8,128)(2,1)}, u32[]{:S(2)}) copy-start(bf16[8,256,512]{2,1,0:T(8,128)(2,1)} %get-tuple-element.23) | copy-start | bytes 6291460
  89.2 1.4 copy-start.5
  94.2 1.4 copy-start.3
  99.4 1.3 copy-start.2
  102.3 29.2 %all-to-all-start.1 = ((f32[64,1,64]{2,1,0:T(1,128)}), f32[64,1,64]{2,1,0:T(1,128)S(1)}, u32[]{:S(2)}, u32[]{:S(2)}) async-start(f32[64,1,64]{2,1,0:T(1,128)} %broadcast_in_dim.42), calls=%async_computation.1 | async-start | bytes 65536 | tf_op jit(solution)/shard_map/all_to_all | solution.py:14
  108.8 23.2 %copy-start.11 = (f32[512]{0:T(512)S(1)}, f32[512]{0:T(512)}, u32[]{:S(2)}) copy-start(f32[512]{0:T(512)} %param.14) | copy-start | bytes 6148
  108.8 23.1 %copy-start.12 = (f32[512]{0:T(512)S(1)}, f32[512]{0:T(512)}, u32[]{:S(2)}) copy-start(f32[512]{0:T(512)} %param.13) | copy-start | bytes 6148
  138.4 1.4 copy-start.8
  142.9 1.4 copy-start.6
  144.3 2.6 %copy-start.4 = (bf16[1,3,512,512]{3,2,1,0:T(8,128)(2,1)S(1)}, bf16[1,3,512,512]{3,2,1,0:T(8,128)(2,1)}, u32[]{:S(2)}) copy-start(bf16[1,3,512,512]{3,2,1,0:T(8,128)(2,1)} %get-tuple-element.9) | copy-start | bytes 4718596
where the time goes:
time: 151 us
  starting transfers between devices  48.5 us (32%)
  waiting for transfers between devices  35.2 us (23%)
  local copies, waits for them, and re-layouts  30.2 us (20%)
  matrix products  22.2 us (15%)
  other arithmetic  14 us (9%)
    all_to_all x2, waiting for transfers between devices, sent_to_all(): return lax.all_to_all(copies, axis, split_axis=0, concat_axis=0, tiled=True)  35.2 us
    all_to_all x2, starting transfers between devices, sent_to_all(): return lax.all_to_all(copies, axis, split_axis=0, concat_axis=0, tiled=True)  24.9 us
    dot_general x9, matrix products, convolve(): jnp.dot(stacked.reshape(height * width, 3 * inputs), kernel[row_shift].re...  22.2 us
    ppermute x1, starting transfers between devices, extended(): lax.ppermute(head, axis, [((i + 1) % count, i) for i in range(ends)])  18.6 us
    slice x3, local copies, waits for them, and re-layouts, convolve(): band[:, col_shift:col_shift + width]  12.5 us
    slice x3, local copies, waits for them, and re-layouts, convolve(): kernel[row_shift].reshape(3 * inputs, -1)  10.2 us
    concatenate x6, other arithmetic, convolve(): jnp.concatenate([band[:, col_shift:col_shift + width] for col_shift in ra...  6.16 us
    select_n x2, other arithmetic, inside(): return jnp.where(valid[:, None, None], field, jnp.zeros_like(field))  5.19 us
  transfers between devices with their start and end apart: 4, of which 2 were waited for; matrix products, arithmetic and copies ran while one was open for 7% of the time, Pallas kernels for 0%

commit v1 on v0

v1 whole, which is shorter than its diff:
```python
import jax
import jax.numpy as jnp
from jax import lax
from jax.experimental import pallas as pl
from jax.experimental.pallas import tpu as pltpu
from jax.sharding import PartitionSpec as P

GROUPS = 32
EPSILON = 1e-06
LANES = 128
HALO = 3
EXACT = lax.Precision.HIGHEST


def dot(a, b):
    return jnp.dot(a, b, preferred_element_type=jnp.float32)


def member(channels, offset, transposed):
    shape = (LANES, channels) if transposed else (channels, LANES)
    channel = lax.broadcasted_iota(jnp.int32, shape, 1 if transposed else 0)
    lane = lax.broadcasted_iota(jnp.int32, shape, 0 if transposed else 1)
    return (channel // (channels // GROUPS) + offset == lane).astype(jnp.float32)


def store_moments(out_ref, sums, squares):
    channels = sums.shape[-1]
    line = jnp.dot(
        jnp.broadcast_to(sums, (8, channels)), member(channels, 0, False), precision=EXACT, preferred_element_type=jnp.float32
    ) + jnp.dot(
        jnp.broadcast_to(squares, (8, channels)), member(channels, GROUPS, False), precision=EXACT, preferred_element_type=jnp.float32
    )
    for at in range(0, out_ref.shape[0], 8):
        out_ref[pl.ds(at, 8), :] = line


def half_affine(all_ref, gain_ref, bias_ref, cells):
    channels = gain_ref.shape[-1]
    count = cells * (channels // GROUPS) * all_ref.shape[0]
    means = jnp.sum(all_ref[...], axis=0, keepdims=True) / count
    means = jnp.broadcast_to(means, (8, LANES))
    center = jnp.dot(means, member(channels, 0, True), precision=EXACT, preferred_element_type=jnp.float32)
    square = jnp.dot(means, member(channels, GROUPS, True), precision=EXACT, preferred_element_type=jnp.float32)
    spread = jnp.maximum(square - center * center, 0.0)
    scale = lax.rsqrt(spread + EPSILON)[0:1] * gain_ref[...]
    shift = bias_ref[...] - center[0:1] * scale
    return scale * 0.5, shift * 0.5


def activate_row(value, scale, shift, inside, x_ref, slot):
    cols, channels = value.shape
    half = value.astype(jnp.float32) * scale + shift
    act = half * jnp.tanh(half) + half
    if inside is not None:
        act = jnp.where(inside, act, 0.0)
    zero = jnp.zeros((1, channels), jnp.float32)
    rows = pl.ds(slot * cols, cols)
    x_ref[rows, 0:channels] = jnp.concatenate([zero, act[:-1]], axis=0).astype(jnp.bfloat16)
    x_ref[rows, channels : 2 * channels] = act.astype(jnp.bfloat16)
    x_ref[rows, 2 * channels :] = jnp.concatenate([act[1:], zero], axis=0).astype(jnp.bfloat16)


def conv_row(x_ref, slot, weight_ref, cols):
    parts = [x_ref[pl.ds((slot + a) * cols, cols), :] for a in range(3)]
    return dot(jnp.concatenate(parts, axis=1), weight_ref[...])


def fill_patches(patch_ref, at, row):
    inputs, cols = row.shape
    values = row.astype(jnp.float32)
    lane = lax.broadcasted_iota(jnp.int32, values.shape, 1)
    left = jnp.where(lane == 0, 0.0, pltpu.roll(values, 1, 1))
    right = jnp.where(lane == cols - 1, 0.0, pltpu.roll(values, cols - 1, 1))
    for b, moved in enumerate((left, values, right)):
        patch_ref[pl.ds((3 * at + b) * inputs, inputs), :] = moved.astype(jnp.bfloat16)


def feature_row(patch_ref, at, inputs, weight):
    patch = patch_ref[pl.ds(3 * at * inputs, 9 * inputs), :]
    return lax.dot_general(patch, weight, (((0,), (0,)), ((), ())), preferred_element_type=jnp.float32).astype(jnp.bfloat16)


def feature_rows(patch_ref, spots, inputs, weight, out_ref):
    sums = squares = 0.0
    for r, at in enumerate(spots):
        rounded = feature_row(patch_ref, at, inputs, weight)
        out_ref[r] = rounded
        values = rounded.astype(jnp.float32)
        sums = sums + jnp.sum(values, axis=0, keepdims=True)
        squares = squares + jnp.sum(values * values, axis=0, keepdims=True)
    return sums, squares


def inner_features(own_ref, weight_ref, out_ref, sums_ref, patch_ref):
    rows, inputs, _ = own_ref.shape
    for at in range(rows):
        fill_patches(patch_ref, at, own_ref[at])
    sums, squares = feature_rows(patch_ref, range(rows - 2), inputs, weight_ref[...], out_ref)
    sums_ref[0:1, :] = sums
    sums_ref[1:2, :] = squares


def outer_features(prev_ref, own_ref, next_ref, weight_ref, sums_ref, out_ref, moments_ref, patch_ref):
    rows, inputs, _ = own_ref.shape
    lines = [prev_ref[HALO - 1], own_ref[0], own_ref[1], own_ref[rows - 2], own_ref[rows - 1], next_ref[0]]
    for at, line in enumerate(lines):
        fill_patches(patch_ref, at, line)
    sums, squares = feature_rows(patch_ref, (0, 3), inputs, weight_ref[...], out_ref)
    store_moments(moments_ref, sums + sums_ref[0:1, :], squares + sums_ref[1:2, :])


def halo_features(prev_ref, own_ref, next_ref, weight_ref, out_ref, patch_ref):
    rows, inputs, _ = own_ref.shape
    lines = [prev_ref[r] for r in range(3)] + [own_ref[0], own_ref[rows - 1]] + [next_ref[r] for r in range(3)]
    for at, line in enumerate(lines):
        fill_patches(patch_ref, at, line)
    weight = weight_ref[...]
    for r, at in enumerate((0, 1, 4, 5)):
        out_ref[r] = feature_row(patch_ref, at, inputs, weight)


def weight_copies(source_ref, weight_ref, sems):
    depth = weight_ref.shape[0] // 3
    return [
        pltpu.make_async_copy(source_ref.at[pl.ds(a * depth, depth)], weight_ref.at[pl.ds(a * depth, depth)], sems.at[a])
        for a in range(3)
    ]


def first_conv_row(x_ref, slot, weight_ref, cols, copies):
    depth = weight_ref.shape[0] // 3
    total = 0.0
    for a, copy in enumerate(copies):
        copy.wait()
        total = total + dot(x_ref[pl.ds((slot + a) * cols, cols), :], weight_ref[pl.ds(a * depth, depth), :])
    return total


def feature_at(inner_ref, outer_ref, r):
    last = inner_ref.shape[0] + 1
    return outer_ref[r // last] if r in (0, last) else inner_ref[r - 1]


def own_hidden(
    edge_ref, inner_ref, outer_ref, halo_ref, all_ref, gain_ref, bias_ref, source_ref, out_ref, moments_ref,
    x_ref, weight_ref, stage_ref, weight_sems, sems,
):
    rows, cols = inner_ref.shape[0] + 2, inner_ref.shape[1]
    weights = weight_copies(source_ref, weight_ref, weight_sems)
    for copy in weights:
        copy.start()
    scale, shift = half_affine(all_ref, gain_ref, bias_ref, rows * cols)
    sums = squares = 0.0

    def fill(slot):
        if slot == 0:
            activate_row(halo_ref[1], scale, shift, edge_ref[0] > 0, x_ref, slot)
        elif slot == rows + 1:
            activate_row(halo_ref[2], scale, shift, edge_ref[1] > 0, x_ref, slot)
        else:
            activate_row(feature_at(inner_ref, outer_ref, slot - 1), scale, shift, None, x_ref, slot)

    for slot in range(3):
        fill(slot)
    copies = []
    for r in range(rows):
        if r:
            fill(r + 2)
        total = conv_row(x_ref, r, weight_ref, cols) if r else first_conv_row(x_ref, r, weight_ref, cols, weights)
        rounded = total.astype(jnp.bfloat16)
        stage_ref[r] = rounded
        copies.append(pltpu.make_async_copy(stage_ref.at[r], out_ref.at[r], sems.at[r]))
        copies[-1].start()
        values = rounded.astype(jnp.float32)
        sums = sums + jnp.sum(values, axis=0, keepdims=True)
        squares = squares + jnp.sum(values * values, axis=0, keepdims=True)
    store_moments(moments_ref, sums, squares)
    for copy in copies:
        copy.wait()


def halo_hidden(
    edge_ref, inner_ref, outer_ref, halo_ref, all_ref, gain_ref, bias_ref, source_ref, out_ref, x_ref, weight_ref, weight_sems
):
    rows, cols = inner_ref.shape[0] + 2, inner_ref.shape[1]
    weights = weight_copies(source_ref, weight_ref, weight_sems)
    for copy in weights:
        copy.start()
    scale, shift = half_affine(all_ref, gain_ref, bias_ref, rows * cols)
    above, below = edge_ref[0] > 0, edge_ref[1] > 0
    activate_row(halo_ref[0], scale, shift, above, x_ref, 0)
    activate_row(halo_ref[1], scale, shift, above, x_ref, 1)
    activate_row(outer_ref[0], scale, shift, None, x_ref, 2)
    out_ref[0] = first_conv_row(x_ref, 0, weight_ref, cols, weights).astype(jnp.bfloat16)
    activate_row(outer_ref[1], scale, shift, None, x_ref, 3)
    activate_row(halo_ref[2], scale, shift, below, x_ref, 4)
    activate_row(halo_ref[3], scale, shift, below, x_ref, 5)
    out_ref[1] = conv_row(x_ref, 3, weight_ref, cols).astype(jnp.bfloat16)


def residual(
    edge_ref, hidden_ref, halo_ref, inner_ref, outer_ref, all_ref, gain_ref, bias_ref, source_ref, out_ref,
    x_ref, weight_ref, own_ref, stage_ref, weight_sems, own_sems, sems,
):
    rows, cols = inner_ref.shape[0] + 2, inner_ref.shape[1]
    loads = [pltpu.make_async_copy(hidden_ref.at[r], own_ref.at[r], own_sems.at[r]) for r in range(rows)]
    weights = weight_copies(source_ref, weight_ref, weight_sems)
    for copy in loads[:2] + weights + loads[2:]:
        copy.start()
    scale, shift = half_affine(all_ref, gain_ref, bias_ref, rows * cols)

    def fill(slot):
        if slot == 0:
            activate_row(halo_ref[0], scale, shift, edge_ref[0] > 0, x_ref, slot)
        elif slot == rows + 1:
            activate_row(halo_ref[1], scale, shift, edge_ref[1] > 0, x_ref, slot)
        else:
            activate_row(own_ref[slot - 1], scale, shift, None, x_ref, slot)

    loads[0].wait()
    loads[1].wait()
    for slot in range(3):
        fill(slot)
    copies = []
    for r in range(rows):
        if r == 1:
            for copy in loads[2:]:
                copy.wait()
        if r:
            fill(r + 2)
        total = conv_row(x_ref, r, weight_ref, cols) if r else first_conv_row(x_ref, r, weight_ref, cols, weights)
        total = feature_at(inner_ref, outer_ref, r).astype(jnp.float32) + total
        stage_ref[r] = total.astype(jnp.bfloat16)
        copies.append(pltpu.make_async_copy(stage_ref.at[r], out_ref.at[r], sems.at[r]))
        copies[-1].start()
    for copy in copies:
        copy.wait()


def call(body, outs, scratch, operands, flops, limit, specs=None, out_specs=None):
    vmem = pl.BlockSpec(memory_space=pltpu.VMEM)
    return pl.pallas_call(
        body,
        out_shape=outs,
        in_specs=specs or [vmem] * len(operands),
        out_specs=out_specs or jax.tree.map(lambda _: vmem, outs),
        scratch_shapes=scratch,
        cost_estimate=pl.CostEstimate(flops=flops, transcendentals=0, bytes_accessed=1 << 20),
        compiler_params=pltpu.CompilerParams(vmem_limit_bytes=limit << 20),
    )(*operands)


def over_all(moments, axis):
    spread = lax.all_to_all(moments[:, None, :], axis, split_axis=0, concat_axis=0, tiled=True)
    return spread[:, 0, :]


def local(latent, kernel_in, gain_one, bias_one, kernel_one, gain_two, bias_two, kernel_two):
    inputs, rows, cols = latent.shape
    channels = kernel_in.shape[-1]
    count = lax.axis_size("rows")
    own = jnp.transpose(latent, (1, 0, 2))
    down = [(i, i + 1) for i in range(count - 1)]
    up = [(i + 1, i) for i in range(count - 1)]
    prev = lax.ppermute(own[rows - HALO :], "rows", down)
    after = lax.ppermute(own[:HALO], "rows", up)
    at = lax.axis_index("rows")
    edge = jnp.stack([at > 0, at < count - 1]).astype(jnp.int32)
    w_in = kernel_in.reshape(9 * inputs, channels)
    w_one = kernel_one.reshape(9 * channels, channels)
    w_two = kernel_two.reshape(9 * channels, channels)
    gain_one, bias_one, gain_two, bias_two = (v[None, :] for v in (gain_one, bias_one, gain_two, bias_two))

    def field(n):
        return jax.ShapeDtypeStruct((n, cols, channels), jnp.bfloat16)

    line = jax.ShapeDtypeStruct((count, LANES), jnp.float32)

    def patches(n):
        return pltpu.VMEM((n * 3 * inputs, cols), jnp.bfloat16)

    def cells(n):
        return pltpu.VMEM((n * cols, 3 * channels), jnp.bfloat16)

    row_flops = 2 * cols * channels * channels * 9
    partial = jax.ShapeDtypeStruct((2, channels), jnp.float32)
    inner, sums = call(inner_features, (field(rows - 2), partial), [patches(rows)], (own, w_in), row_flops, 16)
    latents = (prev, own, after, w_in)
    outer, moments = call(outer_features, (field(2), line), [patches(6)], (*latents, sums), row_flops, 16)
    gathered = over_all(moments, "rows")
    halo = call(halo_features, field(4), [patches(8)], latents, row_flops, 16)

    smem = pl.BlockSpec(memory_space=pltpu.SMEM)
    vmem = pl.BlockSpec(memory_space=pltpu.VMEM)
    away = pl.BlockSpec(memory_space=pl.ANY)
    parts = (edge, inner, outer, halo, gathered, gain_one, bias_one, w_one)
    weight = pltpu.VMEM((9 * channels, channels), jnp.bfloat16)
    stage = pltpu.VMEM((rows, cols, channels), jnp.bfloat16)
    three, six = pltpu.SemaphoreType.DMA((3,)), pltpu.SemaphoreType.DMA((rows,))
    first_specs = [smem] + [vmem] * 6 + [away]
    hidden, moments = call(
        own_hidden,
        (field(rows), line),
        [cells(rows + 2), weight, stage, three, six],
        parts,
        rows * row_flops,
        50,
        first_specs,
        (away, vmem),
    )
    gathered_two = over_all(moments, "rows")
    hidden_halo = call(halo_hidden, field(2), [cells(6), weight, three], parts, 2 * row_flops, 50, first_specs)
    return call(
        residual,
        field(rows),
        [cells(rows + 2), weight, stage, stage, three, six, six],
        (edge, pltpu.with_memory_space_constraint(hidden, pltpu.HBM), hidden_halo, inner, outer, gathered_two, gain_two, bias_two, w_two),
        rows * row_flops,
        50,
        [smem, away] + [vmem] * 6 + [away],
        away,
    )


def solution(mesh):
    in_specs = (P(None, ("batch", "rows"), None), P(), P(), P(), P(), P(), P(), P())
    out_specs = P(("batch", "rows"), None, None)
    return jax.shard_map(local, mesh=mesh, in_specs=in_specs, out_specs=out_specs, check_vma=False)
```

time: 151 us -> 119 us (0.79)
  Pallas kernels: 0 us -> 30.8 us
  local copies, waits for them, and re-layouts: 30.2 us -> 2.55 us
  matrix products: 22.2 us -> 0 us
  other arithmetic: 14 us -> 0.08 us
  waiting for transfers between devices: 35.2 us -> 38.4 us
  starting transfers between devices: 48.5 us -> 46.6 us
    pallas_call x0 -> x6, Pallas kernels: none -> 30.8 us  [call(): pl.pallas_call(body, out_shape=outs, in_specs=specs or [vmem] * len(opera...]
    slice x7 -> x1, local copies, waits for them, and re-layouts: 23.4 us -> 0.81 us  [local(): after = lax.ppermute(own[:HALO], 'rows', up)]
    dot_general x9 -> x0, matrix products: 22.2 us -> none  [convolve(): jnp.dot(stacked.reshape(height * width, 3 * inputs), kernel[row_shift].re...]
    concatenate x8 -> x0, other arithmetic: 6.32 us -> none  [the longest x6 6.16 us: convolve(): jnp.concatenate([band[:, col_shift:col_shift + width] for col_shift in ra...]
    select_n x2 -> x0, other arithmetic: 5.19 us -> none  [inside(): return jnp.where(valid[:, None, None], field, jnp.zeros_like(field))]
    all_to_all x2, waiting for transfers between devices: 35.2 us -> 38.4 us  [over_all(): lax.all_to_all(moments[:, None, :], axis, split_axis=0, concat_axis=0, ti...]
    unnamed x26 -> x16, local copies, waits for them, and re-layouts: 4.51 us -> 1.74 us
    all_to_all x2, starting transfers between devices: 24.9 us -> 22.3 us  [over_all(): lax.all_to_all(moments[:, None, :], axis, split_axis=0, concat_axis=0, ti...]
  transfers between devices with their start and end apart: 4 -> 4, of which waited for: 2 -> 2; matrix products, arithmetic and copies ran while one was open for 7% -> 0% of each run, Pallas kernels for 0% -> 6%
where the time goes in v1:
time: 119 us
  starting transfers between devices  46.6 us (39%)
  waiting for transfers between devices  38.4 us (32%)
  Pallas kernels  30.8 us (26%)
  local copies, waits for them, and re-layouts  2.55 us (2%)
    all_to_all x2, waiting for transfers between devices, over_all(): lax.all_to_all(moments[:, None, :], axis, split_axis=0, concat_axis=0, ti...  38.4 us
    pallas_call x6, Pallas kernels, call(): pl.pallas_call(body, out_shape=outs, in_specs=specs or [vmem] * len(opera...  30.8 us
    ppermute x1, starting transfers between devices, local(): after = lax.ppermute(own[:HALO], 'rows', up)  22.3 us
    all_to_all x2, starting transfers between devices, over_all(): lax.all_to_all(moments[:, None, :], axis, split_axis=0, concat_axis=0, ti...  22.3 us
  transfers between devices with their start and end apart: 4, of which 2 were waited for; matrix products, arithmetic and copies ran while one was open for 0% of the time, Pallas kernels for 6%

profile of v1, /device:TPU:37, one launch (start us, length us, event | category | flops | bytes accessed | tf_op | source)
XLA Modules:
  0.0 118.7 jit_solution(6870765558675349294)
XLA Ops:
  0.0 0.0 copy-start.1
  0.0 0.8 fusion
  0.8 22.3 %collective-permute-start.1 = (bf16[3,16,256]{2,1,0:T(8,128)(2,1)S(1)}, bf16[3,16,256]{2,1,0:T(8,128)(2,1)S(1)}, u32[]{:S(2)}, u32[]{:S(2)}) collective-permute-start(bf16[3,16,256]{2,1,0:T(8,128)(2,1)S(1)} %get-tuple-element.17), channel_id=1, source_target_pairs={{1,0},{2,1},{3,2},{4,3},{5,4},{6,5},{7,6},{8,7},{9,8},{10,9},{11,1... | collective-permute-start | bytes 73736 | tf_op jit(solution)/shard_map/ppermute | solution.py:266
  23.2 2.0 %collective-permute-start = (bf16[3,16,256]{2,1,0:T(8,128)(2,1)S(1)}, bf16[3,16,256]{2,1,0:T(8,128)(2,1)S(1)}, u32[]{:S(2)}, u32[]{:S(2)}) collective-permute-start(bf16[3,16,256]{2,1,0:T(8,128)(2,1)S(1)} %get-tuple-element.18), channel_id=1, source_target_pairs={{0,1},{1,2},{2,3},{3,4},{4,5},{5,6},{6,7},{7,8},{8,9},{9,10},{10,1... | collective-permute-start | bytes 73736 | tf_op jit(solution)/shard_map/ppermute | solution.py:265
  25.1 0.0 copy-start
  25.1 0.8 copy-done
  25.9 0.0 copy-start.2
  25.9 0.9 copy-done.2
  26.8 0.0 copy-start.3
  26.8 0.7 shard_map.82
  27.5 0.0 copy-start.4
  27.6 0.0 copy-start.5
  27.6 0.0 collective-permute-done.1.next_ref
  27.6 0.0 collective-permute-done.prev_ref
  27.6 1.5 %shard_map.83 = (bf16[2,256,512]{2,1,0:T(8,128)(2,1)S(1)}, f32[64,128]{1,0:T(8,128)}) custom-call(bf16[3,16,256]{2,1,0:T(8,128)(2,1)S(1)} %collective-permute-done.prev_ref, bf16[6,16,256]{2,1,0:T(8,128)(2,1)S(1)} %bitcast.20, bf16[3,16,256]{2,1,0:T(8,128)(2,1)S(1)} %collective-permute-done.1.next_ref, bf16[144,512]{1,0:T(8,128)(2,1)S(1)} %bitcast.26, ...), custom_call_target="tpu_custom_call" | custom-call | flops 1207959552 | bytes 1048576 | tf_op jit(solution)/shard_map/pallas_call | solution.py:242
  29.1 15.9 %all-to-all-start = ((f32[64,1,128]{2,1,0:T(1,128)}), f32[64,1,128]{2,1,0:T(1,128)S(1)}, u32[]{:S(2)}, u32[]{:S(2)}) async-start(f32[64,1,128]{2,1,0:T(1,128)} %bitcast.5), calls=%async_computation | async-start | bytes 65536 | tf_op jit(solution)/shard_map/all_to_all | solution.py:254
  45.0 0.1 add_convert_fusion.edge_ref
  45.1 0.0 copy-done.1
  45.1 0.0 copy-done.3
  45.1 0.6 shard_map.84.halo_ref
  45.7 21.1 %all-to-all-done = f32[64,1,128]{2,1,0:T(1,128)S(1)} async-done(((f32[64,1,128]{2,1,0:T(1,128)}), f32[64,1,128]{2,1,0:T(1,128)S(1)}, u32[]{:S(2)}, u32[]{:S(2)}) %all-to-all-start) | async-done | bytes 32800 | tf_op jit(solution)/shard_map/all_to_all | solution.py:254
  66.8 0.0 copy-done.4
  66.8 0.0 copy-done.5
  66.8 11.4 %shard_map.85 = (bf16[6,256,512]{2,1,0:T(8,128)(2,1)}, f32[64,128]{1,0:T(8,128)}) custom-call(s32[2]{0:T(128)S(1)} %add_convert_fusion.edge_ref, bf16[4,256,512]{2,1,0:T(8,128)(2,1)S(1)} %get-tuple-element.11.inner_ref, bf16[2,256,512]{2,1,0:T(8,128)(2,1)S(1)} %get-tuple-element.13.outer_ref, bf16[4,256,512]{2,1,0:T(8,128)(2,1)S(1)} %shard_map.84.halo_ref, ...), custom_call_target="tpu_custom_call" | custom-call | flops 7247757312 | bytes 1048576 | tf_op jit(solution)/shard_map/pallas_call | solution.py:242
  78.2 0.0 copy-start.6
  78.3 0.0 copy-start.7
  78.3 6.4 %all-to-all-start.1 = ((f32[64,1,128]{2,1,0:T(1,128)}), f32[64,1,128]{2,1,0:T(1,128)S(1)}, u32[]{:S(2)}, u32[]{:S(2)}) async-start(f32[64,1,128]{2,1,0:T(1,128)} %bitcast.11), calls=%async_computation.1 | async-start | bytes 65536 | tf_op jit(solution)/shard_map/all_to_all | solution.py:254
  84.7 5.2 %shard_map.86.halo_ref = bf16[2,256,512]{2,1,0:T(8,128)(2,1)S(1)} custom-call(s32[2]{0:T(128)S(1)} %add_convert_fusion.edge_ref, bf16[4,256,512]{2,1,0:T(8,128)(2,1)S(1)} %get-tuple-element.11.inner_ref, bf16[2,256,512]{2,1,0:T(8,128)(2,1)S(1)} %get-tuple-element.13.outer_ref, bf16[4,256,512]{2,1,0:T(8,128)(2,1)S(1)} %shard_map.84.halo_ref, ...), custom_call_target="tpu_custom_call" | custom-call | flops 2415919104 | bytes 1048576 | tf_op jit(solution)/shard_map/pallas_call | solution.py:242
  89.9 17.3 %all-to-all-done.1 = f32[64,1,128]{2,1,0:T(1,128)S(1)} async-done(((f32[64,1,128]{2,1,0:T(1,128)}), f32[64,1,128]{2,1,0:T(1,128)S(1)}, u32[]{:S(2)}, u32[]{:S(2)}) %all-to-all-start.1) | async-done | bytes 32800 | tf_op jit(solution)/shard_map/all_to_all | solution.py:254
  107.2 0.0 copy-done.6
  107.2 0.0 copy-done.7
  107.2 11.3 %shard_map.87 = bf16[6,256,512]{2,1,0:T(8,128)(2,1)} custom-call(s32[2]{0:T(128)S(1)} %add_convert_fusion.edge_ref, bf16[6,256,512]{2,1,0:T(8,128)(2,1)} %get-tuple-element.15.hidden_ref, bf16[2,256,512]{2,1,0:T(8,128)(2,1)S(1)} %shard_map.86.halo_ref, bf16[4,256,512]{2,1,0:T(8,128)(2,1)S(1)} %get-tuple-element.11.inner_ref, ...), custom_call_target="tpu_custom_call" | custom-call | flops 7247757312 | bytes 1048576 | tf_op jit(solution)/shard_map/pallas_call | solution.py:242
Async XLA Ops:
  0.0 45.1 %copy-start.1 = (bf16[16,6,256]{2,0,1:T(8,128)(2,1)S(1)}, bf16[16,6,256]{2,0,1:T(8,128)(2,1)}, u32[]{:S(2)}) copy-start(bf16[16,6,256]{2,0,1:T(8,128)(2,1)} %param.8) | copy-start | bytes 147460
  0.8 26.8 %collective-permute-start.1 = (bf16[3,16,256]{2,1,0:T(8,128)(2,1)S(1)}, bf16[3,16,256]{2,1,0:T(8,128)(2,1)S(1)}, u32[]{:S(2)}, u32[]{:S(2)}) collective-permute-start(bf16[3,16,256]{2,1,0:T(8,128)(2,1)S(1)} %get-tuple-element.17), channel_id=1, source_target_pairs={{1,0},{2,1},{3,2},{4,3},{5,4},{6,5},{7,6},{8,7},{9,8},{10,9},{11,1... | collective-permute-start | bytes 73736 | tf_op jit(solution)/shard_map/ppermute | solution.py:266
  23.2 4.4 %collective-permute-start = (bf16[3,16,256]{2,1,0:T(8,128)(2,1)S(1)}, bf16[3,16,256]{2,1,0:T(8,128)(2,1)S(1)}, u32[]{:S(2)}, u32[]{:S(2)}) collective-permute-start(bf16[3,16,256]{2,1,0:T(8,128)(2,1)S(1)} %get-tuple-element.18), channel_id=1, source_target_pairs={{0,1},{1,2},{2,3},{3,4},{4,5},{5,6},{6,7},{7,8},{8,9},{9,10},{10,1... | collective-permute-start | bytes 73736 | tf_op jit(solution)/shard_map/ppermute | solution.py:265
  25.1 0.8 copy-start
  25.9 0.9 copy-start.2
  26.8 18.2 %copy-start.3 = (bf16[3,3,16,512]{3,2,1,0:T(8,128)(2,1)S(1)}, bf16[3,3,16,512]{3,2,1,0:T(8,128)(2,1)}, u32[]{:S(2)}) copy-start(bf16[3,3,16,512]{3,2,1,0:T(8,128)(2,1)} %param.9) | copy-start | bytes 442372
  27.5 39.3 %copy-start.4 = (f32[512]{0:T(512)S(1)}, f32[512]{0:T(512)}, u32[]{:S(2)}) copy-start(f32[512]{0:T(512)} %param.10) | copy-start | bytes 6148
  27.6 39.3 %copy-start.5 = (f32[512]{0:T(512)S(1)}, f32[512]{0:T(512)}, u32[]{:S(2)}) copy-start(f32[512]{0:T(512)} %param.11) | copy-start | bytes 6148
  29.1 37.7 %all-to-all-start = ((f32[64,1,128]{2,1,0:T(1,128)}), f32[64,1,128]{2,1,0:T(1,128)S(1)}, u32[]{:S(2)}, u32[]{:S(2)}) async-start(f32[64,1,128]{2,1,0:T(1,128)} %bitcast.5), calls=%async_computation | async-start | bytes 65536 | tf_op jit(solution)/shard_map/all_to_all | solution.py:254
  78.2 29.0 %copy-start.6 = (f32[512]{0:T(512)S(1)}, f32[512]{0:T(512)}, u32[]{:S(2)}) copy-start(f32[512]{0:T(512)} %param.13) | copy-start | bytes 6148
  78.3 29.0 %copy-start.7 = (f32[512]{0:T(512)S(1)}, f32[512]{0:T(512)}, u32[]{:S(2)}) copy-start(f32[512]{0:T(512)} %param.14) | copy-start | bytes 6148
  78.3 28.9 %all-to-all-start.1 = ((f32[64,1,128]{2,1,0:T(1,128)}), f32[64,1,128]{2,1,0:T(1,128)S(1)}, u32[]{:S(2)}, u32[]{:S(2)}) async-start(f32[64,1,128]{2,1,0:T(1,128)} %bitcast.11), calls=%async_computation.1 | async-start | bytes 65536 | tf_op jit(solution)/shard_map/all_to_all | solution.py:254

commit v2 on v1

--- a/solution.py
+++ b/solution.py
@@ -9,27 +9,36 @@
 EPSILON = 1e-06
 LANES = 128
 HALO = 3
-EXACT = lax.Precision.HIGHEST
+BURSTS = (3, 5)
 
 
 def dot(a, b):
     return jnp.dot(a, b, preferred_element_type=jnp.float32)
 
 
-def member(channels, offset, transposed):
-    shape = (LANES, channels) if transposed else (channels, LANES)
-    channel = lax.broadcasted_iota(jnp.int32, shape, 1 if transposed else 0)
-    lane = lax.broadcasted_iota(jnp.int32, shape, 0 if transposed else 1)
-    return (channel // (channels // GROUPS) + offset == lane).astype(jnp.float32)
+def split(values):
+    high = values.astype(jnp.bfloat16).astype(jnp.float32)
+    rest = values - high
+    middle = rest.astype(jnp.bfloat16).astype(jnp.float32)
+    return [high, middle, rest - middle]
+
+
+def partial_sums(values):
+    cells, channels = values.shape
+    return jnp.sum(values.reshape(cells // 8, 8, channels), axis=0)
 
 
 def store_moments(out_ref, sums, squares):
     channels = sums.shape[-1]
-    line = jnp.dot(
-        jnp.broadcast_to(sums, (8, channels)), member(channels, 0, False), precision=EXACT, preferred_element_type=jnp.float32
-    ) + jnp.dot(
-        jnp.broadcast_to(squares, (8, channels)), member(channels, GROUPS, False), precision=EXACT, preferred_element_type=jnp.float32
-    )
+    channel = lax.broadcasted_iota(jnp.int32, (channels, LANES), 0)
+    lane = lax.broadcasted_iota(jnp.int32, (channels, LANES), 1)
+    member = (channel // (channels // GROUPS) == lane % GROUPS).astype(jnp.bfloat16)
+    terms = jnp.concatenate(split(sums) + split(squares), axis=0).astype(jnp.bfloat16)
+    totals = dot(terms, member)
+    half = totals.shape[0] // 2
+    first = jnp.sum(totals[:half], axis=0, keepdims=True)
+    second = jnp.sum(totals[half:], axis=0, keepdims=True)
+    line = jnp.where(lax.broadcasted_iota(jnp.int32, (8, LANES), 1) < GROUPS, first, second)
     for at in range(0, out_ref.shape[0], 8):
         out_ref[pl.ds(at, 8), :] = line
 
@@ -37,13 +46,18 @@
 def half_affine(all_ref, gain_ref, bias_ref, cells):
     channels = gain_ref.shape[-1]
     count = cells * (channels // GROUPS) * all_ref.shape[0]
-    means = jnp.sum(all_ref[...], axis=0, keepdims=True) / count
-    means = jnp.broadcast_to(means, (8, LANES))
-    center = jnp.dot(means, member(channels, 0, True), precision=EXACT, preferred_element_type=jnp.float32)
-    square = jnp.dot(means, member(channels, GROUPS, True), precision=EXACT, preferred_element_type=jnp.float32)
+    channel = lax.broadcasted_iota(jnp.int32, (LANES, channels), 1) // (channels // GROUPS)
+    lane = lax.broadcasted_iota(jnp.int32, (LANES, channels), 0)
+    terms = jnp.concatenate(split(partial_sums(all_ref[...])), axis=0).astype(jnp.bfloat16)
+
+    def mean(offset):
+        member = (channel + offset == lane).astype(jnp.bfloat16)
+        return jnp.sum(dot(terms, member), axis=0, keepdims=True) / count
+
+    center, square = mean(0), mean(GROUPS)
     spread = jnp.maximum(square - center * center, 0.0)
-    scale = lax.rsqrt(spread + EPSILON)[0:1] * gain_ref[...]
-    shift = bias_ref[...] - center[0:1] * scale
+    scale = lax.rsqrt(spread + EPSILON) * gain_ref[...]
+    shift = bias_ref[...] - center * scale
     return scale * 0.5, shift * 0.5
 
 
@@ -86,8 +100,8 @@
         rounded = feature_row(patch_ref, at, inputs, weight)
         out_ref[r] = rounded
         values = rounded.astype(jnp.float32)
-        sums = sums + jnp.sum(values, axis=0, keepdims=True)
-        squares = squares + jnp.sum(values * values, axis=0, keepdims=True)
+        sums = sums + partial_sums(values)
+        squares = squares + partial_sums(values * values)
     return sums, squares
 
 
@@ -96,8 +110,8 @@
     for at in range(rows):
         fill_patches(patch_ref, at, own_ref[at])
     sums, squares = feature_rows(patch_ref, range(rows - 2), inputs, weight_ref[...], out_ref)
-    sums_ref[0:1, :] = sums
-    sums_ref[1:2, :] = squares
+    sums_ref[0] = sums
+    sums_ref[1] = squares
 
 
 def outer_features(prev_ref, own_ref, next_ref, weight_ref, sums_ref, out_ref, moments_ref, patch_ref):
@@ -106,7 +120,7 @@
     for at, line in enumerate(lines):
         fill_patches(patch_ref, at, line)
     sums, squares = feature_rows(patch_ref, (0, 3), inputs, weight_ref[...], out_ref)
-    store_moments(moments_ref, sums + sums_ref[0:1, :], squares + sums_ref[1:2, :])
+    store_moments(moments_ref, sums + sums_ref[0], squares + sums_ref[1])
 
 
 def halo_features(prev_ref, own_ref, next_ref, weight_ref, out_ref, patch_ref):
@@ -134,6 +148,13 @@
         copy.wait()
         total = total + dot(x_ref[pl.ds((slot + a) * cols, cols), :], weight_ref[pl.ds(a * depth, depth), :])
     return total
+
+
+def start_rows(stage_ref, out_ref, sems, first, end):
+    copies = [pltpu.make_async_copy(stage_ref.at[r], out_ref.at[r], sems.at[r]) for r in range(first, end)]
+    for copy in copies:
+        copy.start()
+    return copies
 
 
 def feature_at(inner_ref, outer_ref, r):
@@ -169,11 +190,11 @@
         total = conv_row(x_ref, r, weight_ref, cols) if r else first_conv_row(x_ref, r, weight_ref, cols, weights)
         rounded = total.astype(jnp.bfloat16)
         stage_ref[r] = rounded
-        copies.append(pltpu.make_async_copy(stage_ref.at[r], out_ref.at[r], sems.at[r]))
-        copies[-1].start()
         values = rounded.astype(jnp.float32)
-        sums = sums + jnp.sum(values, axis=0, keepdims=True)
-        squares = squares + jnp.sum(values * values, axis=0, keepdims=True)
+        sums = sums + partial_sums(values)
+        squares = squares + partial_sums(values * values)
+        if r in BURSTS:
+            copies += start_rows(stage_ref, out_ref, sems, len(copies), r + 1)
     store_moments(moments_ref, sums, squares)
     for copy in copies:
         copy.wait()
@@ -231,8 +252,8 @@
         total = conv_row(x_ref, r, weight_ref, cols) if r else first_conv_row(x_ref, r, weight_ref, cols, weights)
         total = feature_at(inner_ref, outer_ref, r).astype(jnp.float32) + total
         stage_ref[r] = total.astype(jnp.bfloat16)
-        copies.append(pltpu.make_async_copy(stage_ref.at[r], out_ref.at[r], sems.at[r]))
-        copies[-1].start()
+        if r in BURSTS:
+            copies += start_rows(stage_ref, out_ref, sems, len(copies), r + 1)
     for copy in copies:
         copy.wait()
 
@@ -283,7 +304,7 @@
         return pltpu.VMEM((n * cols, 3 * channels), jnp.bfloat16)
 
     row_flops = 2 * cols * channels * channels * 9
-    partial = jax.ShapeDtypeStruct((2, channels), jnp.float32)
+    partial = jax.ShapeDtypeStruct((2, 8, channels), jnp.float32)
     inner, sums = call(inner_features, (field(rows - 2), partial), [patches(rows)], (own, w_in), row_flops, 16)
     latents = (prev, own, after, w_in)
     outer, moments = call(outer_features, (field(2), line), [patches(6)], (*latents, sums), row_flops, 16)

time: 119 us -> 119 us (level)
  transfers between devices with their start and end apart: 4 -> 4, of which waited for: 2 -> 2; matrix products, arithmetic and copies ran while one was open for 0% -> 0% of each run, Pallas kernels for 6% -> 5%
where the time goes in v2:
time: 119 us
  starting transfers between devices  46.6 us (39%)
  waiting for transfers between devices  38.5 us (32%)
  Pallas kernels  30.8 us (26%)
  local copies, waits for them, and re-layouts  2.55 us (2%)
    all_to_all x2, waiting for transfers between devices, over_all(): lax.all_to_all(moments[:, None, :], axis, split_axis=0, concat_axis=0, ti...  38.5 us
    pallas_call x6, Pallas kernels, call(): pl.pallas_call(body, out_shape=outs, in_specs=specs or [vmem] * len(opera...  30.8 us
    ppermute x1, starting transfers between devices, local(): after = lax.ppermute(own[:HALO], 'rows', up)  22.3 us
    all_to_all x2, starting transfers between devices, over_all(): lax.all_to_all(moments[:, None, :], axis, split_axis=0, concat_axis=0, ti...  22.3 us
  transfers between devices with their start and end apart: 4, of which 2 were waited for; matrix products, arithmetic and copies ran while one was open for 0% of the time, Pallas kernels for 5%

profile of v2, /device:TPU:37, one launch (start us, length us, event | category | flops | bytes accessed | tf_op | source)
XLA Modules:
  0.0 118.8 jit_solution(12846558900628812523)
XLA Ops:
  0.0 0.0 copy-start.1
  0.0 0.8 fusion
  0.8 22.3 %collective-permute-start.1 = (bf16[3,16,256]{2,1,0:T(8,128)(2,1)S(1)}, bf16[3,16,256]{2,1,0:T(8,128)(2,1)S(1)}, u32[]{:S(2)}, u32[]{:S(2)}) collective-permute-start(bf16[3,16,256]{2,1,0:T(8,128)(2,1)S(1)} %get-tuple-element.17), channel_id=1, source_target_pairs={{1,0},{2,1},{3,2},{4,3},{5,4},{6,5},{7,6},{8,7},{9,8},{10,9},{11,1... | collective-permute-start | bytes 73736 | tf_op jit(solution)/shard_map/ppermute | solution.py:287
  23.2 2.0 %collective-permute-start = (bf16[3,16,256]{2,1,0:T(8,128)(2,1)S(1)}, bf16[3,16,256]{2,1,0:T(8,128)(2,1)S(1)}, u32[]{:S(2)}, u32[]{:S(2)}) collective-permute-start(bf16[3,16,256]{2,1,0:T(8,128)(2,1)S(1)} %get-tuple-element.18), channel_id=1, source_target_pairs={{0,1},{1,2},{2,3},{3,4},{4,5},{5,6},{6,7},{7,8},{8,9},{9,10},{10,1... | collective-permute-start | bytes 73736 | tf_op jit(solution)/shard_map/ppermute | solution.py:286
  25.1 0.0 copy-start
  25.1 0.8 copy-done
  25.9 0.0 copy-start.2
  25.9 0.9 copy-done.2
  26.8 0.0 copy-start.3
  26.8 0.7 shard_map.82
  27.5 0.0 copy-start.4
  27.5 0.0 copy-start.5
  27.5 0.0 collective-permute-done.1.next_ref
  27.6 0.0 collective-permute-done.prev_ref
  27.6 1.3 %shard_map.83 = (bf16[2,256,512]{2,1,0:T(8,128)(2,1)S(1)}, f32[64,128]{1,0:T(8,128)}) custom-call(bf16[3,16,256]{2,1,0:T(8,128)(2,1)S(1)} %collective-permute-done.prev_ref, bf16[6,16,256]{2,1,0:T(8,128)(2,1)S(1)} %bitcast.20, bf16[3,16,256]{2,1,0:T(8,128)(2,1)S(1)} %collective-permute-done.1.next_ref, bf16[144,512]{1,0:T(8,128)(2,1)S(1)} %bitcast.26, ...), custom_call_target="tpu_custom_call" | custom-call | flops 1207959552 | bytes 1048576 | tf_op jit(solution)/shard_map/pallas_call | solution.py:263
  28.8 15.9 %all-to-all-start = ((f32[64,1,128]{2,1,0:T(1,128)}), f32[64,1,128]{2,1,0:T(1,128)S(1)}, u32[]{:S(2)}, u32[]{:S(2)}) async-start(f32[64,1,128]{2,1,0:T(1,128)} %bitcast.5), calls=%async_computation | async-start | bytes 65536 | tf_op jit(solution)/shard_map/all_to_all | solution.py:275
  44.7 0.1 add_convert_fusion.edge_ref
  44.8 0.0 copy-done.1
  44.8 0.0 copy-done.3
  44.8 0.6 shard_map.84.halo_ref
  45.5 21.1 %all-to-all-done = f32[64,1,128]{2,1,0:T(1,128)S(1)} async-done(((f32[64,1,128]{2,1,0:T(1,128)}), f32[64,1,128]{2,1,0:T(1,128)S(1)}, u32[]{:S(2)}, u32[]{:S(2)}) %all-to-all-start) | async-done | bytes 32800 | tf_op jit(solution)/shard_map/all_to_all | solution.py:275
  66.6 0.0 copy-done.4
  66.6 0.0 copy-done.5
  66.6 11.7 %shard_map.85 = (bf16[6,256,512]{2,1,0:T(8,128)(2,1)}, f32[64,128]{1,0:T(8,128)}) custom-call(s32[2]{0:T(128)S(1)} %add_convert_fusion.edge_ref, bf16[4,256,512]{2,1,0:T(8,128)(2,1)S(1)} %get-tuple-element.11.inner_ref, bf16[2,256,512]{2,1,0:T(8,128)(2,1)S(1)} %get-tuple-element.13.outer_ref, bf16[4,256,512]{2,1,0:T(8,128)(2,1)S(1)} %shard_map.84.halo_ref, ...), custom_call_target="tpu_custom_call" | custom-call | flops 7247757312 | bytes 1048576 | tf_op jit(solution)/shard_map/pallas_call | solution.py:263
  78.3 0.0 copy-start.6
  78.3 0.0 copy-start.7
  78.3 6.4 %all-to-all-start.1 = ((f32[64,1,128]{2,1,0:T(1,128)}), f32[64,1,128]{2,1,0:T(1,128)S(1)}, u32[]{:S(2)}, u32[]{:S(2)}) async-start(f32[64,1,128]{2,1,0:T(1,128)} %bitcast.11), calls=%async_computation.1 | async-start | bytes 65536 | tf_op jit(solution)/shard_map/all_to_all | solution.py:275
  84.7 5.1 %shard_map.86.halo_ref = bf16[2,256,512]{2,1,0:T(8,128)(2,1)S(1)} custom-call(s32[2]{0:T(128)S(1)} %add_convert_fusion.edge_ref, bf16[4,256,512]{2,1,0:T(8,128)(2,1)S(1)} %get-tuple-element.11.inner_ref, bf16[2,256,512]{2,1,0:T(8,128)(2,1)S(1)} %get-tuple-element.13.outer_ref, bf16[4,256,512]{2,1,0:T(8,128)(2,1)S(1)} %shard_map.84.halo_ref, ...), custom_call_target="tpu_custom_call" | custom-call | flops 2415919104 | bytes 1048576 | tf_op jit(solution)/shard_map/pallas_call | solution.py:263
  89.9 17.4 %all-to-all-done.1 = f32[64,1,128]{2,1,0:T(1,128)S(1)} async-done(((f32[64,1,128]{2,1,0:T(1,128)}), f32[64,1,128]{2,1,0:T(1,128)S(1)}, u32[]{:S(2)}, u32[]{:S(2)}) %all-to-all-start.1) | async-done | bytes 32800 | tf_op jit(solution)/shard_map/all_to_all | solution.py:275
  107.2 0.0 copy-done.6
  107.2 0.0 copy-done.7
  107.2 11.4 %shard_map.87 = bf16[6,256,512]{2,1,0:T(8,128)(2,1)} custom-call(s32[2]{0:T(128)S(1)} %add_convert_fusion.edge_ref, bf16[6,256,512]{2,1,0:T(8,128)(2,1)} %get-tuple-element.15.hidden_ref, bf16[2,256,512]{2,1,0:T(8,128)(2,1)S(1)} %shard_map.86.halo_ref, bf16[4,256,512]{2,1,0:T(8,128)(2,1)S(1)} %get-tuple-element.11.inner_ref, ...), custom_call_target="tpu_custom_call" | custom-call | flops 7247757312 | bytes 1048576 | tf_op jit(solution)/shard_map/pallas_call | solution.py:263
Async XLA Ops:
  0.0 44.8 %copy-start.1 = (bf16[16,6,256]{2,0,1:T(8,128)(2,1)S(1)}, bf16[16,6,256]{2,0,1:T(8,128)(2,1)}, u32[]{:S(2)}) copy-start(bf16[16,6,256]{2,0,1:T(8,128)(2,1)} %param.8) | copy-start | bytes 147460
  0.8 26.7 %collective-permute-start.1 = (bf16[3,16,256]{2,1,0:T(8,128)(2,1)S(1)}, bf16[3,16,256]{2,1,0:T(8,128)(2,1)S(1)}, u32[]{:S(2)}, u32[]{:S(2)}) collective-permute-start(bf16[3,16,256]{2,1,0:T(8,128)(2,1)S(1)} %get-tuple-element.17), channel_id=1, source_target_pairs={{1,0},{2,1},{3,2},{4,3},{5,4},{6,5},{7,6},{8,7},{9,8},{10,9},{11,1... | collective-permute-start | bytes 73736 | tf_op jit(solution)/shard_map/ppermute | solution.py:287
  23.2 4.4 %collective-permute-start = (bf16[3,16,256]{2,1,0:T(8,128)(2,1)S(1)}, bf16[3,16,256]{2,1,0:T(8,128)(2,1)S(1)}, u32[]{:S(2)}, u32[]{:S(2)}) collective-permute-start(bf16[3,16,256]{2,1,0:T(8,128)(2,1)S(1)} %get-tuple-element.18), channel_id=1, source_target_pairs={{0,1},{1,2},{2,3},{3,4},{4,5},{5,6},{6,7},{7,8},{8,9},{9,10},{10,1... | collective-permute-start | bytes 73736 | tf_op jit(solution)/shard_map/ppermute | solution.py:286
  25.1 0.8 copy-start
  25.9 0.9 copy-start.2
  26.8 18.0 %copy-start.3 = (bf16[3,3,16,512]{3,2,1,0:T(8,128)(2,1)S(1)}, bf16[3,3,16,512]{3,2,1,0:T(8,128)(2,1)}, u32[]{:S(2)}) copy-start(bf16[3,3,16,512]{3,2,1,0:T(8,128)(2,1)} %param.9) | copy-start | bytes 442372
  27.5 39.1 %copy-start.4 = (f32[512]{0:T(512)S(1)}, f32[512]{0:T(512)}, u32[]{:S(2)}) copy-start(f32[512]{0:T(512)} %param.10) | copy-start | bytes 6148
  27.5 39.0 %copy-start.5 = (f32[512]{0:T(512)S(1)}, f32[512]{0:T(512)}, u32[]{:S(2)}) copy-start(f32[512]{0:T(512)} %param.11) | copy-start | bytes 6148
  28.8 37.8 %all-to-all-start = ((f32[64,1,128]{2,1,0:T(1,128)}), f32[64,1,128]{2,1,0:T(1,128)S(1)}, u32[]{:S(2)}, u32[]{:S(2)}) async-start(f32[64,1,128]{2,1,0:T(1,128)} %bitcast.5), calls=%async_computation | async-start | bytes 65536 | tf_op jit(solution)/shard_map/all_to_all | solution.py:275
  78.3 29.0 %copy-start.6 = (f32[512]{0:T(512)S(1)}, f32[512]{0:T(512)}, u32[]{:S(2)}) copy-start(f32[512]{0:T(512)} %param.13) | copy-start | bytes 6148
  78.3 28.9 %copy-start.7 = (f32[512]{0:T(512)S(1)}, f32[512]{0:T(512)}, u32[]{:S(2)}) copy-start(f32[512]{0:T(512)} %param.14) | copy-start | bytes 6148
  78.3 28.9 %all-to-all-start.1 = ((f32[64,1,128]{2,1,0:T(1,128)}), f32[64,1,128]{2,1,0:T(1,128)S(1)}, u32[]{:S(2)}, u32[]{:S(2)}) async-start(f32[64,1,128]{2,1,0:T(1,128)} %bitcast.11), calls=%async_computation.1 | async-start | bytes 65536 | tf_op jit(solution)/shard_map/all_to_all | solution.py:275

commit v3 on v2

--- a/solution.py
+++ b/solution.py
@@ -133,11 +133,22 @@
         out_ref[r] = feature_row(patch_ref, at, inputs, weight)
 
 
-def weight_copies(source_ref, weight_ref, sems):
-    depth = weight_ref.shape[0] // 3
+def mixed_taps(taps_ref, _, out_ref):
+    taps = [taps_ref[a].astype(jnp.float32) * 0.5 for a in range(3)]
+    ends = taps[0] + taps[2]
+    out_ref[0] = (ends + taps[1]).astype(jnp.bfloat16)
+    out_ref[1] = (ends - taps[1]).astype(jnp.bfloat16)
+
+
+def four_taps(source_ref, mixed_ref):
+    depth = source_ref.shape[0] // 3
+    return [source_ref.at[pl.ds(0, depth)], mixed_ref.at[0], mixed_ref.at[1], source_ref.at[pl.ds(2 * depth, depth)]]
+
+
+def weight_copies(sources, weight_ref, sems):
+    depth = weight_ref.shape[0] // len(sources)
     return [
-        pltpu.make_async_copy(source_ref.at[pl.ds(a * depth, depth)], weight_ref.at[pl.ds(a * depth, depth)], sems.at[a])
-        for a in range(3)
+        pltpu.make_async_copy(source, weight_ref.at[pl.ds(a * depth, depth)], sems.at[a]) for a, source in enumerate(sources)
     ]
 
 
@@ -150,6 +161,21 @@
     return total
 
 
+def conv_pair(x_ref, slot, weight_ref, cols, copies, m_ref):
+    depth = weight_ref.shape[0] // 4
+
+    def product(k, sign, near, far):
+        if copies:
+            copies[k].wait()
+        left = x_ref[pl.ds((slot + near) * cols, cols), :]
+        right = x_ref[pl.ds((slot + far) * cols, cols), :]
+        return dot(left + right if sign > 0 else left - right, weight_ref[pl.ds(k * depth, depth), :])
+
+    for k, sign, near, far in ((0, -1, 0, 2), (1, 1, 1, 2), (2, -1, 2, 1), (3, -1, 1, 3)):
+        m_ref[k] = product(k, sign, near, far)
+    return m_ref[0] + m_ref[1] + m_ref[2], m_ref[1] - m_ref[2] - m_ref[3]
+
+
 def start_rows(stage_ref, out_ref, sems, first, end):
     copies = [pltpu.make_async_copy(stage_ref.at[r], out_ref.at[r], sems.at[r]) for r in range(first, end)]
     for copy in copies:
@@ -167,7 +193,8 @@
     x_ref, weight_ref, stage_ref, weight_sems, sems,
 ):
     rows, cols = inner_ref.shape[0] + 2, inner_ref.shape[1]
-    weights = weight_copies(source_ref, weight_ref, weight_sems)
+    depth = weight_ref.shape[0] // 3
+    weights = weight_copies([source_ref.at[pl.ds(a * depth, depth)] for a in range(3)], weight_ref, weight_sems)
     for copy in weights:
         copy.start()
     scale, shift = half_affine(all_ref, gain_ref, bias_ref, rows * cols)
@@ -204,7 +231,8 @@
     edge_ref, inner_ref, outer_ref, halo_ref, all_ref, gain_ref, bias_ref, source_ref, out_ref, x_ref, weight_ref, weight_sems
 ):
     rows, cols = inner_ref.shape[0] + 2, inner_ref.shape[1]
-    weights = weight_copies(source_ref, weight_ref, weight_sems)
+    depth = weight_ref.shape[0] // 3
+    weights = weight_copies([source_ref.at[pl.ds(a * depth, depth)] for a in range(3)], weight_ref, weight_sems)
     for copy in weights:
         copy.start()
     scale, shift = half_affine(all_ref, gain_ref, bias_ref, rows * cols)
@@ -220,13 +248,13 @@
 
 
 def residual(
-    edge_ref, hidden_ref, halo_ref, inner_ref, outer_ref, all_ref, gain_ref, bias_ref, source_ref, out_ref,
-    x_ref, weight_ref, own_ref, stage_ref, weight_sems, own_sems, sems,
+    edge_ref, hidden_ref, halo_ref, inner_ref, outer_ref, all_ref, gain_ref, bias_ref, source_ref, mixed_ref, out_ref,
+    x_ref, weight_ref, own_ref, stage_ref, m_ref, weight_sems, own_sems, sems,
 ):
     rows, cols = inner_ref.shape[0] + 2, inner_ref.shape[1]
     loads = [pltpu.make_async_copy(hidden_ref.at[r], own_ref.at[r], own_sems.at[r]) for r in range(rows)]
-    weights = weight_copies(source_ref, weight_ref, weight_sems)
-    for copy in loads[:2] + weights + loads[2:]:
+    weights = weight_copies(four_taps(source_ref, mixed_ref), weight_ref, weight_sems)
+    for copy in loads[:3] + weights + loads[3:]:
         copy.start()
     scale, shift = half_affine(all_ref, gain_ref, bias_ref, rows * cols)
 
@@ -238,22 +266,22 @@
         else:
             activate_row(own_ref[slot - 1], scale, shift, None, x_ref, slot)
 
-    loads[0].wait()
-    loads[1].wait()
-    for slot in range(3):
-        fill(slot)
+    for copy in loads[:3]:
+        copy.wait()
+    fill(0)
+    fill(1)
     copies = []
-    for r in range(rows):
-        if r == 1:
-            for copy in loads[2:]:
+    for r in range(0, rows, 2):
+        if r == 2:
+            for copy in loads[3:]:
                 copy.wait()
-        if r:
-            fill(r + 2)
-        total = conv_row(x_ref, r, weight_ref, cols) if r else first_conv_row(x_ref, r, weight_ref, cols, weights)
-        total = feature_at(inner_ref, outer_ref, r).astype(jnp.float32) + total
-        stage_ref[r] = total.astype(jnp.bfloat16)
-        if r in BURSTS:
-            copies += start_rows(stage_ref, out_ref, sems, len(copies), r + 1)
+        fill(r + 2)
+        fill(r + 3)
+        for k, total in enumerate(conv_pair(x_ref, r, weight_ref, cols, [] if r else weights, m_ref)):
+            total = feature_at(inner_ref, outer_ref, r + k).astype(jnp.float32) + total
+            stage_ref[r + k] = total.astype(jnp.bfloat16)
+        if r + 1 in BURSTS:
+            copies += start_rows(stage_ref, out_ref, sems, len(copies), r + 2)
     for copy in copies:
         copy.wait()
 
@@ -269,6 +297,23 @@
         cost_estimate=pl.CostEstimate(flops=flops, transcendentals=0, bytes_accessed=1 << 20),
         compiler_params=pltpu.CompilerParams(vmem_limit_bytes=limit << 20),
     )(*operands)
+
+
+def mixed(kernel, after):
+    depth, channels = 3 * kernel.shape[-2], kernel.shape[-1]
+    block = depth // 6
+    return pl.pallas_call(
+        mixed_taps,
+        out_shape=jax.ShapeDtypeStruct((2, depth, channels), jnp.bfloat16),
+        grid=(6,),
+        in_specs=[
+            pl.BlockSpec((3, block, channels), lambda i: (0, i, 0)),
+            pl.BlockSpec(memory_space=pl.ANY),
+        ],
+        out_specs=pl.BlockSpec((2, block, channels), lambda i: (0, i, 0)),
+        cost_estimate=pl.CostEstimate(flops=1 << 31, transcendentals=0, bytes_accessed=8 << 20),
+        compiler_params=pltpu.CompilerParams(vmem_limit_bytes=50 << 20),
+    )(kernel.reshape(3, depth, channels), after)
 
 
 def over_all(moments, axis):
@@ -317,6 +362,9 @@
     parts = (edge, inner, outer, halo, gathered, gain_one, bias_one, w_one)
     weight = pltpu.VMEM((9 * channels, channels), jnp.bfloat16)
     stage = pltpu.VMEM((rows, cols, channels), jnp.bfloat16)
+    four_weights = pltpu.VMEM((12 * channels, channels), jnp.bfloat16)
+    products = pltpu.VMEM((4, cols, channels), jnp.float32)
+    four = pltpu.SemaphoreType.DMA((4,))
     three, six = pltpu.SemaphoreType.DMA((3,)), pltpu.SemaphoreType.DMA((rows,))
     first_specs = [smem] + [vmem] * 6 + [away]
     hidden, moments = call(
@@ -331,14 +379,15 @@
     )
     gathered_two = over_all(moments, "rows")
     hidden_halo = call(halo_hidden, field(2), [cells(6), weight, three], parts, 2 * row_flops, 50, first_specs)
+    mixed_two = mixed(kernel_two, hidden_halo)
     return call(
         residual,
         field(rows),
-        [cells(rows + 2), weight, stage, stage, three, six, six],
-        (edge, pltpu.with_memory_space_constraint(hidden, pltpu.HBM), hidden_halo, inner, outer, gathered_two, gain_two, bias_two, w_two),
+        [cells(rows + 2), four_weights, stage, stage, products, four, six, six],
+        (edge, pltpu.with_memory_space_constraint(hidden, pltpu.HBM), hidden_halo, inner, outer, gathered_two, gain_two, bias_two, w_two, mixed_two),
         rows * row_flops,
         50,
-        [smem, away] + [vmem] * 6 + [away],
+        [smem, away] + [vmem] * 6 + [away] * 2,
         away,
     )
 

time: 119 us -> 118 us (level)
  waiting for transfers between devices: 38.5 us -> 32.3 us
  Pallas kernels: 30.8 us -> 33.7 us
  local copies, waits for them, and re-layouts: 2.55 us -> 4.13 us
    all_to_all x2, waiting for transfers between devices: 38.5 us -> 32.3 us  [over_all(): lax.all_to_all(moments[:, None, :], axis, split_axis=0, concat_axis=0, ti...]
    pallas_call x0 -> x1, Pallas kernels: none -> 4.46 us  [mixed(): pl.pallas_call(mixed_taps, out_shape=jax.ShapeDtypeStruct((2, depth, chan...]
    unnamed x16 -> x18, local copies, waits for them, and re-layouts: 1.74 us -> 3.37 us
    pallas_call x6, Pallas kernels: 30.8 us -> 29.3 us  [call(): pl.pallas_call(body, out_shape=outs, in_specs=specs or [vmem] * len(opera...]
  transfers between devices with their start and end apart: 4 -> 4, of which waited for: 2 -> 2; matrix products, arithmetic and copies ran while one was open for 0% -> 0% of each run, Pallas kernels for 5% -> 9%
where the time goes in v3:
time: 118 us; the launch traced here: 117 us
  starting transfers between devices  46.8 us (40%)
  Pallas kernels  33.7 us (29%)
  waiting for transfers between devices  32.3 us (27%)
  local copies, waits for them, and re-layouts  4.13 us (4%)
    all_to_all x2, waiting for transfers between devices, over_all(): lax.all_to_all(moments[:, None, :], axis, split_axis=0, concat_axis=0, ti...  32.3 us
    pallas_call x6, Pallas kernels, call(): pl.pallas_call(body, out_shape=outs, in_specs=specs or [vmem] * len(opera...  29.3 us
    all_to_all x2, starting transfers between devices, over_all(): lax.all_to_all(moments[:, None, :], axis, split_axis=0, concat_axis=0, ti...  22.5 us
    ppermute x1, starting transfers between devices, local(): after = lax.ppermute(own[:HALO], 'rows', up)  22.3 us
    pallas_call x1, Pallas kernels, mixed(): pl.pallas_call(mixed_taps, out_shape=jax.ShapeDtypeStruct((2, depth, chan...  4.46 us
    unnamed x18, local copies, waits for them, and re-layouts  3.37 us
  transfers between devices with their start and end apart: 4, of which 2 were waited for; matrix products, arithmetic and copies ran while one was open for 0% of the time, Pallas kernels for 9%

profile of v3, /device:TPU:37, one launch (start us, length us, event | category | flops | bytes accessed | tf_op | source)
XLA Modules:
  0.0 117.3 jit_solution(17989907932587456781)
XLA Ops:
  0.0 0.8 fusion
  0.8 22.3 %collective-permute-start.1 = (bf16[3,16,256]{2,1,0:T(8,128)(2,1)S(1)}, bf16[3,16,256]{2,1,0:T(8,128)(2,1)S(1)}, u32[]{:S(2)}, u32[]{:S(2)}) collective-permute-start(bf16[3,16,256]{2,1,0:T(8,128)(2,1)S(1)} %get-tuple-element.17), channel_id=1, source_target_pairs={{1,0},{2,1},{3,2},{4,3},{5,4},{6,5},{7,6},{8,7},{9,8},{10,9},{11,1... | collective-permute-start | bytes 73736 | tf_op jit(solution)/shard_map/ppermute | solution.py:332
  23.1 2.0 %collective-permute-start = (bf16[3,16,256]{2,1,0:T(8,128)(2,1)S(1)}, bf16[3,16,256]{2,1,0:T(8,128)(2,1)S(1)}, u32[]{:S(2)}, u32[]{:S(2)}) collective-permute-start(bf16[3,16,256]{2,1,0:T(8,128)(2,1)S(1)} %get-tuple-element.18), channel_id=1, source_target_pairs={{0,1},{1,2},{2,3},{3,4},{4,5},{5,6},{6,7},{7,8},{8,9},{9,10},{10,1... | collective-permute-start | bytes 73736 | tf_op jit(solution)/shard_map/ppermute | solution.py:331
  25.1 0.0 copy-start.1
  25.1 0.8 copy-done.1
  25.9 0.9 copy-done.3
  26.8 0.7 shard_map.82
  27.5 0.0 copy-start.2
  27.5 0.0 copy-start.4
  27.5 0.0 collective-permute-done.1.next_ref
  27.5 0.0 collective-permute-done.prev_ref
  27.5 1.3 %shard_map.83 = (bf16[2,256,512]{2,1,0:T(8,128)(2,1)S(1)}, f32[64,128]{1,0:T(8,128)}) custom-call(bf16[3,16,256]{2,1,0:T(8,128)(2,1)S(1)} %collective-permute-done.prev_ref, bf16[6,16,256]{2,1,0:T(8,128)(2,1)S(1)} %bitcast.21, bf16[3,16,256]{2,1,0:T(8,128)(2,1)S(1)} %collective-permute-done.1.next_ref, bf16[144,512]{1,0:T(8,128)(2,1)S(1)} %bitcast.27, ...), custom_call_target="tpu_custom_call" | custom-call | flops 1207959552 | bytes 1048576 | tf_op jit(solution)/shard_map/pallas_call | solution.py:291
  28.8 16.0 %all-to-all-start = ((f32[64,1,128]{2,1,0:T(1,128)}), f32[64,1,128]{2,1,0:T(1,128)S(1)}, u32[]{:S(2)}, u32[]{:S(2)}) async-start(f32[64,1,128]{2,1,0:T(1,128)} %bitcast.5), calls=%async_computation | async-start | bytes 65536 | tf_op jit(solution)/shard_map/all_to_all | solution.py:320
  44.8 0.1 add_convert_fusion.edge_ref
  44.9 0.0 copy-done.2
  44.9 0.0 copy-done.4
  44.9 0.6 shard_map.84.halo_ref
  45.5 21.1 %all-to-all-done = f32[64,1,128]{2,1,0:T(1,128)S(1)} async-done(((f32[64,1,128]{2,1,0:T(1,128)}), f32[64,1,128]{2,1,0:T(1,128)S(1)}, u32[]{:S(2)}, u32[]{:S(2)}) %all-to-all-start) | async-done | bytes 32800 | tf_op jit(solution)/shard_map/all_to_all | solution.py:320
  66.7 0.0 copy-done.5
  66.7 0.0 copy-done.6
  66.7 11.7 %shard_map.85 = (bf16[6,256,512]{2,1,0:T(8,128)(2,1)}, f32[64,128]{1,0:T(8,128)}) custom-call(s32[2]{0:T(128)S(1)} %add_convert_fusion.edge_ref, bf16[4,256,512]{2,1,0:T(8,128)(2,1)S(1)} %get-tuple-element.11.inner_ref, bf16[2,256,512]{2,1,0:T(8,128)(2,1)S(1)} %get-tuple-element.13.outer_ref, bf16[4,256,512]{2,1,0:T(8,128)(2,1)S(1)} %shard_map.84.halo_ref, ...), custom_call_target="tpu_custom_call" | custom-call | flops 7247757312 | bytes 1048576 | tf_op jit(solution)/shard_map/pallas_call | solution.py:291
  78.3 6.4 %all-to-all-start.1 = ((f32[64,1,128]{2,1,0:T(1,128)}), f32[64,1,128]{2,1,0:T(1,128)S(1)}, u32[]{:S(2)}, u32[]{:S(2)}) async-start(f32[64,1,128]{2,1,0:T(1,128)} %bitcast.11), calls=%async_computation.1 | async-start | bytes 65536 | tf_op jit(solution)/shard_map/all_to_all | solution.py:320
  84.8 5.1 %shard_map.86._.halo_ref = bf16[2,256,512]{2,1,0:T(8,128)(2,1)S(1)} custom-call(s32[2]{0:T(128)S(1)} %add_convert_fusion.edge_ref, bf16[4,256,512]{2,1,0:T(8,128)(2,1)S(1)} %get-tuple-element.11.inner_ref, bf16[2,256,512]{2,1,0:T(8,128)(2,1)S(1)} %get-tuple-element.13.outer_ref, bf16[4,256,512]{2,1,0:T(8,128)(2,1)S(1)} %shard_map.84.halo_ref, ...), custom_call_target="tpu_custom_call" | custom-call | flops 2415919104 | bytes 1048576 | tf_op jit(solution)/shard_map/pallas_call | solution.py:291
  89.9 0.0 copy-start.7
  89.9 0.0 copy-start.8
  89.9 4.5 %shard_map.87.mixed_ref = bf16[2,1536,512]{2,1,0:T(8,128)(2,1)S(1)} custom-call(bf16[3,1536,512]{2,1,0:T(8,128)(2,1)} %bitcast.35, bf16[2,256,512]{2,1,0:T(8,128)(2,1)S(1)} %shard_map.86._.halo_ref), custom_call_target="tpu_custom_call" | custom-call | flops 2147483648 | bytes 8388608 | tf_op jit(solution)/shard_map/pallas_call | solution.py:305
  94.4 0.0 copy-start
  94.4 1.6 %copy-done = bf16[2,1536,512]{2,1,0:T(8,128)(2,1)} copy-done((bf16[2,1536,512]{2,1,0:T(8,128)(2,1)}, bf16[2,1536,512]{2,1,0:T(8,128)(2,1)S(1)}, u32[]{:S(2)}) %copy-start) | copy-done | bytes 3145752
  96.1 11.2 %all-to-all-done.1 = f32[64,1,128]{2,1,0:T(1,128)S(1)} async-done(((f32[64,1,128]{2,1,0:T(1,128)}), f32[64,1,128]{2,1,0:T(1,128)S(1)}, u32[]{:S(2)}, u32[]{:S(2)}) %all-to-all-start.1) | async-done | bytes 32800 | tf_op jit(solution)/shard_map/all_to_all | solution.py:320
  107.3 0.0 copy-done.7
  107.3 0.0 copy-done.8
  107.3 9.9 %shard_map.88 = bf16[6,256,512]{2,1,0:T(8,128)(2,1)} custom-call(s32[2]{0:T(128)S(1)} %add_convert_fusion.edge_ref, bf16[6,256,512]{2,1,0:T(8,128)(2,1)} %get-tuple-element.15.hidden_ref, bf16[2,256,512]{2,1,0:T(8,128)(2,1)S(1)} %shard_map.86._.halo_ref, bf16[4,256,512]{2,1,0:T(8,128)(2,1)S(1)} %get-tuple-element.11.inner_ref, ...), custom_call_target="tpu_custom_call" | custom-call | flops 7247757312 | bytes 1048576 | tf_op jit(solution)/shard_map/pallas_call | solution.py:291
  (3 shorter events, 0.0 us)
Async XLA Ops:
  0.8 26.7 %collective-permute-start.1 = (bf16[3,16,256]{2,1,0:T(8,128)(2,1)S(1)}, bf16[3,16,256]{2,1,0:T(8,128)(2,1)S(1)}, u32[]{:S(2)}, u32[]{:S(2)}) collective-permute-start(bf16[3,16,256]{2,1,0:T(8,128)(2,1)S(1)} %get-tuple-element.17), channel_id=1, source_target_pairs={{1,0},{2,1},{3,2},{4,3},{5,4},{6,5},{7,6},{8,7},{9,8},{10,9},{11,1... | collective-permute-start | bytes 73736 | tf_op jit(solution)/shard_map/ppermute | solution.py:332
  23.1 4.4 %collective-permute-start = (bf16[3,16,256]{2,1,0:T(8,128)(2,1)S(1)}, bf16[3,16,256]{2,1,0:T(8,128)(2,1)S(1)}, u32[]{:S(2)}, u32[]{:S(2)}) collective-permute-start(bf16[3,16,256]{2,1,0:T(8,128)(2,1)S(1)} %get-tuple-element.18), channel_id=1, source_target_pairs={{0,1},{1,2},{2,3},{3,4},{4,5},{5,6},{6,7},{7,8},{8,9},{9,10},{10,1... | collective-permute-start | bytes 73736 | tf_op jit(solution)/shard_map/ppermute | solution.py:331
  25.1 0.8 copy-start.1
  25.9 0.9 copy-start.3
  27.5 17.4 %copy-start.2 = (bf16[16,6,256]{2,0,1:T(8,128)(2,1)S(1)}, bf16[16,6,256]{2,0,1:T(8,128)(2,1)}, u32[]{:S(2)}) copy-start(bf16[16,6,256]{2,0,1:T(8,128)(2,1)} %param.8) | copy-start | bytes 147460
  27.5 17.4 %copy-start.4 = (bf16[3,3,16,512]{3,2,1,0:T(8,128)(2,1)S(1)}, bf16[3,3,16,512]{3,2,1,0:T(8,128)(2,1)}, u32[]{:S(2)}) copy-start(bf16[3,3,16,512]{3,2,1,0:T(8,128)(2,1)} %param.9) | copy-start | bytes 442372
  28.8 37.9 %copy-start.5 = (f32[512]{0:T(512)S(1)}, f32[512]{0:T(512)}, u32[]{:S(2)}) copy-start(f32[512]{0:T(512)} %param.10) | copy-start | bytes 6148
  28.8 37.9 %copy-start.6 = (f32[512]{0:T(512)S(1)}, f32[512]{0:T(512)}, u32[]{:S(2)}) copy-start(f32[512]{0:T(512)} %param.11) | copy-start | bytes 6148
  28.8 37.9 %all-to-all-start = ((f32[64,1,128]{2,1,0:T(1,128)}), f32[64,1,128]{2,1,0:T(1,128)S(1)}, u32[]{:S(2)}, u32[]{:S(2)}) async-start(f32[64,1,128]{2,1,0:T(1,128)} %bitcast.5), calls=%async_computation | async-start | bytes 65536 | tf_op jit(solution)/shard_map/all_to_all | solution.py:320
  78.3 28.9 %all-to-all-start.1 = ((f32[64,1,128]{2,1,0:T(1,128)}), f32[64,1,128]{2,1,0:T(1,128)S(1)}, u32[]{:S(2)}, u32[]{:S(2)}) async-start(f32[64,1,128]{2,1,0:T(1,128)} %bitcast.11), calls=%async_computation.1 | async-start | bytes 65536 | tf_op jit(solution)/shard_map/all_to_all | solution.py:320
  89.9 17.4 %copy-start.7 = (f32[512]{0:T(512)S(1)}, f32[512]{0:T(512)}, u32[]{:S(2)}) copy-start(f32[512]{0:T(512)} %param.13) | copy-start | bytes 6148
  89.9 17.3 %copy-start.8 = (f32[512]{0:T(512)S(1)}, f32[512]{0:T(512)}, u32[]{:S(2)}) copy-start(f32[512]{0:T(512)} %param.14) | copy-start | bytes 6148
  94.4 1.6 %copy-start = (bf16[2,1536,512]{2,1,0:T(8,128)(2,1)}, bf16[2,1536,512]{2,1,0:T(8,128)(2,1)S(1)}, u32[]{:S(2)}) copy-start(bf16[2,1536,512]{2,1,0:T(8,128)(2,1)S(1)} %shard_map.87.mixed_ref) | copy-start | bytes 9437188
